TPU v7x, 32 devices: a whole 2x2x4 slice. The times are simulated.
32 devices in a mesh: ctx: 8 (over z, x), head: 4 (over y, core).
Axes of the slice: x: 2, y: 2, z: 4, core: 2. Of those that a mesh axis runs over, the one named last changes fastest.
Arguments:
- queries: bfloat16 [2048, 2048], P(('ctx', 'head')), may hold values from -6 to 6
- key_vectors_state: bfloat16 [2048, 512], P(('ctx', 'head')), may hold values from -6 to 6
- value_vectors_state: bfloat16 [2048, 512], P(('ctx', 'head')), may hold values from -6 to 6
- doc_bounds: int32 [17], replicated, may hold values from 0 to 2048, as said below
Outputs:
- attended: bfloat16 [2048, 2048], P(('ctx', 'head'))
Inputs may be any that keep to these rules, and one draw needn't show every extreme that they name: doc_bounds[0] is 0 and doc_bounds[16] is 2048; the entries strictly increase, and doc_bounds[1] to doc_bounds[15] all lie below 1024, so the last document holds at least half of the tokens.
All inputs are finite; a program needn't handle non-finite values.
Results may differ from a plain program's by a relative error of at most 0.004.
Values may be sent and summed in bfloat16 or wider, within the bound.
A program may use at most 64 MiB of HBM per device.

v0:
```python
import math

import jax
import jax.numpy as jnp
from jax import lax
from jax.sharding import PartitionSpec as P

QUERY_HEADS = 32
KEY_VALUE_HEADS = 8
HEAD_SIZE = 64


masked_score = -1e30


def from_behind(block, axis, distance):
    devices = range(lax.axis_size(axis))
    route = [((i - distance) % len(devices), i) for i in devices]
    return lax.ppermute(block, axis, route)


def document_of(positions, doc_bounds):
    interior = doc_bounds[1:-1]
    return jnp.sum((interior[None, :] <= positions[:, None]).astype(jnp.int32), axis=1)


def on_device(queries, key_vectors_state, value_vectors_state, doc_bounds):
    query_loc, key_loc, value_loc = (
        lax.all_to_all(queries, "head", split_axis=1, concat_axis=0, tiled=True),
        lax.all_to_all(key_vectors_state, "head", split_axis=1, concat_axis=0, tiled=True),
        lax.all_to_all(value_vectors_state, "head", split_axis=1, concat_axis=0, tiled=True),
    )
    tok_rows = query_loc.shape[0]
    cycle_size = lax.axis_size("ctx")
    my_index = lax.axis_index("ctx")
    kv_local = key_loc.shape[1] // HEAD_SIZE
    queries_per_group = QUERY_HEADS // KEY_VALUE_HEADS
    score_scale = 1.0 / math.sqrt(HEAD_SIZE)
    first_pos = my_index * tok_rows
    query_pos = first_pos + jnp.arange(tok_rows, dtype=jnp.int32)
    heads_of_queries = query_loc.reshape(tok_rows, kv_local, queries_per_group, HEAD_SIZE)
    query_doc = document_of(query_pos, doc_bounds)

    def attend(running, key_piece, value_piece, anchor):
        key_count = key_piece.shape[0]
        key_pos = anchor + jnp.arange(key_count, dtype=jnp.int32)
        key_doc = document_of(key_pos, doc_bounds)
        allowed = (
            (query_doc[:, None] == key_doc[None, :])
            & (key_pos[None, :] <= query_pos[:, None])
            & (key_pos[None, :] >= 0)
        )
        heads_of_keys = key_piece.reshape(key_count, kv_local, HEAD_SIZE)
        heads_of_values = value_piece.reshape(key_count, kv_local, HEAD_SIZE)
        run_max, run_sum, weighted = running
        scores = (
            jnp.einsum(
                "qgjd,kgd->qgjk",
                heads_of_queries,
                heads_of_keys,
                preferred_element_type=jnp.float32,
            )
            * score_scale
        )
        visible = allowed[:, None, None, :]
        masked = jnp.where(visible, scores, masked_score)
        new_max = jnp.maximum(run_max, jnp.max(masked, axis=-1))
        weights = jnp.exp(masked - new_max[..., None]) * visible.astype(jnp.float32)
        shrink = jnp.exp(run_max - new_max)
        new_sum = run_sum * shrink + jnp.sum(weights, axis=-1)
        rounded = weights.astype(jnp.bfloat16)
        mixed = jnp.einsum(
            "qgjk,kgd->qgjd", rounded, heads_of_values, preferred_element_type=jnp.float32
        )
        return (new_max, new_sum, weighted * shrink[..., None] + mixed)

    def fold_keys(running, key_piece, value_piece, anchor):
        key_count = key_piece.shape[0]
        return attend(running, key_piece, value_piece, anchor)

    stat_shape = (tok_rows, kv_local, queries_per_group)
    initial = (
        jnp.full(stat_shape, masked_score, jnp.float32),
        jnp.zeros(stat_shape, jnp.float32),
        jnp.zeros((tok_rows, kv_local, queries_per_group, HEAD_SIZE), jnp.float32),
    )
    bound_heads = doc_bounds[:-1]
    doc_start = jnp.max(
        jnp.where(bound_heads[None, :] <= query_pos[:, None], bound_heads[None, :], 0), axis=1
    )
    start_block = doc_start // tok_rows
    own_block = query_pos // tok_rows
    row_turns = jnp.where(
        own_block <= my_index,
        my_index - start_block,
        jnp.where(start_block <= my_index, cycle_size - 1, my_index - start_block + cycle_size),
    )
    reach_steps = lax.pmax(jnp.max(row_turns), "ctx")
    running = fold_keys(initial, key_loc, value_loc, first_pos)

    def cycle_turn(turn_index, state):
        paired, inner_state = state
        paired = from_behind(paired, "ctx", 1)
        anchor = jnp.mod(my_index - turn_index - 1, cycle_size) * tok_rows
        return (paired, fold_keys(inner_state, paired[0], paired[1], anchor))

    stacked = jnp.stack((key_loc, value_loc))
    stacked, running = lax.fori_loop(0, reach_steps, cycle_turn, (stacked, running))
    run_max, run_sum, weighted = running
    attended = (
        (weighted / run_sum[..., None])
        .astype(jnp.bfloat16)
        .reshape(tok_rows, kv_local * queries_per_group * HEAD_SIZE)
    )
    return lax.all_to_all(attended, "head", split_axis=0, concat_axis=1, tiled=True)


def solution(mesh):
    return jax.shard_map(
        on_device,
        mesh=mesh,
        in_specs=(
            P(("ctx", "head"), None),
            P(("ctx", "head"), None),
            P(("ctx", "head"), None),
            P(),
        ),
        out_specs=P(("ctx", "head"), None),
        check_vma=False,
    )
```

profile of v0, /device:TPU:0, one launch (start us, length us, event | category | flops | bytes accessed | tf_op | source)
XLA Modules:
  0.0 87.6 jit_solution(5063558174066637305)
XLA Ops:
  0.0 0.8 copy-done
  0.8 0.6 copy_bitcast_fusion.2
  1.5 4.3 %all-to-all-start = ((bf16[64,4,128]{2,0,1:T(8,128)(2,1)}), bf16[64,4,128]{2,0,1:T(8,128)(2,1)S(1)}, u32[]{:S(2)}, u32[]{:S(2)}) async-start(bf16[64,4,128]{2,0,1:T(8,128)(2,1)} %copy_bitcast_fusion.2), calls=%async_computation | async-start | bytes 131072 | tf_op jit(solution)/shard_map/all_to_all | solution.py:30
  5.7 0.7 slice.25
  6.6 0.7 select_reduce_fusion
  7.3 1.5 %copy_bitcast_fusion.1 = bf16[64,4,128]{2,0,1:T(8,128)(2,1)} fusion(bf16[64,512]{1,0:T(8,128)(2,1)} %param.8), kind=kLoop, calls=%fused_computation.40 | loop fusion | bytes 131072 | tf_op jit(solution)/shard_map/all_to_all | solution.py:31
  8.8 0.6 fusion.26
  9.9 3.3 %all-to-all-start.1 = ((bf16[64,4,128]{2,0,1:T(8,128)(2,1)}), bf16[64,4,128]{2,0,1:T(8,128)(2,1)S(1)}, u32[]{:S(2)}, u32[]{:S(2)}) async-start(bf16[64,4,128]{2,0,1:T(8,128)(2,1)} %copy_bitcast_fusion.1), calls=%async_computation.1 | async-start | bytes 131072 | tf_op jit(solution)/shard_map/all_to_all | solution.py:31
  13.2 1.7 %copy.82 = bf16[8,4,8,512]{3,2,0,1:T(8,128)(2,1)} copy(bf16[8,4,8,512]{3,2,1,0:T(8,128)(2,1)} %bitcast.126) | data formatting | bytes 524288 | tf_op jit(solution)/shard_map/all_to_all | solution.py:29
  14.8 2.4 %all-to-all-done.1 = bf16[64,4,128]{2,0,1:T(8,128)(2,1)S(1)} async-done(((bf16[64,4,128]{2,0,1:T(8,128)(2,1)}), bf16[64,4,128]{2,0,1:T(8,128)(2,1)S(1)}, u32[]{:S(2)}, u32[]{:S(2)}) %all-to-all-start.1) | async-done | bytes 65568 | tf_op jit(solution)/shard_map/all_to_all | solution.py:31
  17.2 3.4 %all-to-all-start.2 = ((bf16[64,4,512]{2,0,1:T(8,128)(2,1)}), bf16[64,4,512]{2,0,1:T(8,128)(2,1)S(1)}, u32[]{:S(2)}, u32[]{:S(2)}) async-start(bf16[64,4,512]{2,0,1:T(8,128)(2,1)} %bitcast.73), calls=%async_computation.2 | async-start | bytes 524288 | tf_op jit(solution)/shard_map/all_to_all | solution.py:29
  20.8 12.6 %pmax.7 = s32[]{:T(128)} all-reduce(s32[]{:T(128)} %fusion.26), channel_id=1, replica_groups=mesh['ctx'=8,'head'=4] {'ctx'}, use_global_device_ids=true, to_apply=%region_5.6 | all-reduce | flops 1 | bytes 8 | tf_op jit(solution)/shard_map/pmax | solution.py:98
  34.9 0.5 fusion.16
  35.4 0.7 fusion.17
  36.2 41.1 %while.19 = (s32[]{:T(128)}, bf16[2,256,128]{1,2,0:T(8,128)(2,1)S(1)}, f32[256,2,4]{0,2,1:T(4,128)S(1)}, f32[256,2,4]{0,2,1:T(4,128)S(1)}, f32[256,2,4,64]{0,3,2...) while((s32[]{:T(128)}, ...), condition=%wide.region_10.11_spmd.clone, body=%wide.region_6.10_spmd.clone.sunk | while | flops 141639696 | bytes 9970710 | solution.py:108
  36.7 1.5 %collective-permute-start = (bf16[2,256,128]{1,2,0:T(8,128)(2,1)S(1)}, bf16[2,256,128]{1,2,0:T(8,128)(2,1)S(1)}, u32[]{:S(2)}, u32[]{:S(2)}) collective-permute-start(bf16[2,256,128]{1,2,0:T(8,128)(2,1)S(1)} %get-tuple-element.362), channel_id=1, source_target_pairs={{28,0},{0,4},{4,8},{8,12},{12,16},{16,20},{20,24},{24,28},{29,1},{... | collective-permute-start | bytes 393224 | tf_op jit(solution)/shard_map/while/body/ppermute | solution.py:19
  38.7 5.8 %collective-permute-done = bf16[2,256,128]{1,2,0:T(8,128)(2,1)S(1)} collective-permute-done((bf16[2,256,128]{1,2,0:T(8,128)(2,1)S(1)}, bf16[2,256,128]{1,2,0:T(8,128)(2,1)S(1)}, u32[]{:S(2)}, u32[]{:S(2)}) %collective-permute-start) | collective-permute-done | bytes 131104 | tf_op jit(solution)/shard_map/while/body/ppermute | solution.py:19
  44.5 0.5 fusion.54
  45.0 0.5 fusion.55
  45.5 0.7 fusion.56
  47.3 7.3 %collective-permute-done = bf16[2,256,128]{1,2,0:T(8,128)(2,1)S(1)} collective-permute-done((bf16[2,256,128]{1,2,0:T(8,128)(2,1)S(1)}, bf16[2,256,128]{1,2,0:T(8,128)(2,1)S(1)}, u32[]{:S(2)}, u32[]{:S(2)}) %collective-permute-start) | collective-permute-done | bytes 131104 | tf_op jit(solution)/shard_map/while/body/ppermute | solution.py:19
  55.1 0.5 fusion.55
  55.7 0.7 fusion.56
  57.5 7.3 %collective-permute-done = bf16[2,256,128]{1,2,0:T(8,128)(2,1)S(1)} collective-permute-done((bf16[2,256,128]{1,2,0:T(8,128)(2,1)S(1)}, bf16[2,256,128]{1,2,0:T(8,128)(2,1)S(1)}, u32[]{:S(2)}, u32[]{:S(2)}) %collective-permute-start) | collective-permute-done | bytes 131104 | tf_op jit(solution)/shard_map/while/body/ppermute | solution.py:19
  64.7 0.5 fusion.54
  65.2 0.5 fusion.55
  65.8 0.7 fusion.56
  67.6 7.3 %collective-permute-done = bf16[2,256,128]{1,2,0:T(8,128)(2,1)S(1)} collective-permute-done((bf16[2,256,128]{1,2,0:T(8,128)(2,1)S(1)}, bf16[2,256,128]{1,2,0:T(8,128)(2,1)S(1)}, u32[]{:S(2)}, u32[]{:S(2)}) %collective-permute-start) | collective-permute-done | bytes 131104 | tf_op jit(solution)/shard_map/while/body/ppermute | solution.py:19
  75.4 0.5 fusion.55
  75.9 0.7 fusion.56
  77.9 9.1 %all_to_all.67 = bf16[4,64,512]{2,1,0:T(8,128)(2,1)S(1)} all-to-all(bf16[4,64,512]{2,1,0:T(8,128)(2,1)S(1)} %copy.68), channel_id=1, replica_groups=mesh['ctx'=8,'head'=4] {'head'}, dimensions={0} | all-to-all | bytes 524288 | tf_op jit(solution)/shard_map/all_to_all | solution.py:115
  86.9 0.7 copy.72
  (70 shorter events, 5.4 us)
Async XLA Ops:
  0.0 0.8 copy-start
  1.5 8.4 %all-to-all-start = ((bf16[64,4,128]{2,0,1:T(8,128)(2,1)}), bf16[64,4,128]{2,0,1:T(8,128)(2,1)S(1)}, u32[]{:S(2)}, u32[]{:S(2)}) async-start(bf16[64,4,128]{2,0,1:T(8,128)(2,1)} %copy_bitcast_fusion.2), calls=%async_computation | async-start | bytes 131072 | tf_op jit(solution)/shard_map/all_to_all | solution.py:30
  9.9 7.4 %all-to-all-start.1 = ((bf16[64,4,128]{2,0,1:T(8,128)(2,1)}), bf16[64,4,128]{2,0,1:T(8,128)(2,1)S(1)}, u32[]{:S(2)}, u32[]{:S(2)}) async-start(bf16[64,4,128]{2,0,1:T(8,128)(2,1)} %copy_bitcast_fusion.1), calls=%async_computation.1 | async-start | bytes 131072 | tf_op jit(solution)/shard_map/all_to_all | solution.py:31
  17.2 16.5 %all-to-all-start.2 = ((bf16[64,4,512]{2,0,1:T(8,128)(2,1)}), bf16[64,4,512]{2,0,1:T(8,128)(2,1)S(1)}, u32[]{:S(2)}, u32[]{:S(2)}) async-start(bf16[64,4,512]{2,0,1:T(8,128)(2,1)} %bitcast.73), calls=%async_computation.2 | async-start | bytes 524288 | tf_op jit(solution)/shard_map/all_to_all | solution.py:29
  35.4 0.8 copy-start.1
  36.7 7.7 %collective-permute-start = (bf16[2,256,128]{1,2,0:T(8,128)(2,1)S(1)}, bf16[2,256,128]{1,2,0:T(8,128)(2,1)S(1)}, u32[]{:S(2)}, u32[]{:S(2)}) collective-permute-start(bf16[2,256,128]{1,2,0:T(8,128)(2,1)S(1)} %get-tuple-element.362), channel_id=1, source_target_pairs={{28,0},{0,4},{4,8},{8,12},{12,16},{16,20},{20,24},{24,28},{29,1},{... | collective-permute-start | bytes 393224 | tf_op jit(solution)/shard_map/while/body/ppermute | solution.py:19
  46.9 7.7 %collective-permute-start = (bf16[2,256,128]{1,2,0:T(8,128)(2,1)S(1)}, bf16[2,256,128]{1,2,0:T(8,128)(2,1)S(1)}, u32[]{:S(2)}, u32[]{:S(2)}) collective-permute-start(bf16[2,256,128]{1,2,0:T(8,128)(2,1)S(1)} %get-tuple-element.362), channel_id=1, source_target_pairs={{28,0},{0,4},{4,8},{8,12},{12,16},{16,20},{20,24},{24,28},{29,1},{... | collective-permute-start | bytes 393224 | tf_op jit(solution)/shard_map/while/body/ppermute | solution.py:19
  57.0 7.7 %collective-permute-start = (bf16[2,256,128]{1,2,0:T(8,128)(2,1)S(1)}, bf16[2,256,128]{1,2,0:T(8,128)(2,1)S(1)}, u32[]{:S(2)}, u32[]{:S(2)}) collective-permute-start(bf16[2,256,128]{1,2,0:T(8,128)(2,1)S(1)} %get-tuple-element.362), channel_id=1, source_target_pairs={{28,0},{0,4},{4,8},{8,12},{12,16},{16,20},{20,24},{24,28},{29,1},{... | collective-permute-start | bytes 393224 | tf_op jit(solution)/shard_map/while/body/ppermute | solution.py:19
  67.1 7.7 %collective-permute-start = (bf16[2,256,128]{1,2,0:T(8,128)(2,1)S(1)}, bf16[2,256,128]{1,2,0:T(8,128)(2,1)S(1)}, u32[]{:S(2)}, u32[]{:S(2)}) collective-permute-start(bf16[2,256,128]{1,2,0:T(8,128)(2,1)S(1)} %get-tuple-element.362), channel_id=1, source_target_pairs={{28,0},{0,4},{4,8},{8,12},{12,16},{16,20},{20,24},{24,28},{29,1},{... | collective-permute-start | bytes 393224 | tf_op jit(solution)/shard_map/while/body/ppermute | solution.py:19
where the time goes:
time: 88.2 us; the launch traced here: 87.6 us
  waiting for transfers between devices  30.4 us (34%)
  blocking collectives  21.7 us (25%)
  starting transfers between devices  12.7 us (14%)
  local copies, waits for them, and re-layouts  7.91 us (9%)
  matrix products  6.12 us (7%)
  other arithmetic  5.49 us (6%)
  loops' own time  3.19 us (4%)
    ppermute x4, waiting for transfers between devices, from_behind(): return lax.ppermute(block, axis, route)  27.6 us
    pmax x1, blocking collectives, on_device(): reach_steps = lax.pmax(jnp.max(row_turns), 'ctx')  12.6 us
    all_to_all x1, blocking collectives, on_device(): lax.all_to_all(attended, 'head', split_axis=0, concat_axis=1, tiled=True)  9.06 us
    all_to_all x1, starting transfers between devices, on_device(): lax.all_to_all(key_vectors_state, 'head', split_axis=1, concat_axis=0, ti...  4.26 us
    dot_general x5, matrix products, attend(): jnp.einsum('qgjk,kgd->qgjd', rounded, heads_of_values, preferred_element_...  3.68 us
    all_to_all x1, starting transfers between devices, on_device(): lax.all_to_all(queries, 'head', split_axis=1, concat_axis=0, tiled=True)  3.41 us
    all_to_all x1, starting transfers between devices, on_device(): lax.all_to_all(value_vectors_state, 'head', split_axis=1, concat_axis=0,...  3.28 us
    another operation x1, loops' own time, on_device(): lax.fori_loop(0, reach_steps, cycle_turn, (stacked, running))  3.19 us
  transfers between devices with their start and end apart: 7, of which 6 were waited for; matrix products, arithmetic and copies ran while one was open for 8% of the time, Pallas kernels for 0%

commit v1 on v0

v1 whole, which is shorter than its diff:
```python
import functools
import math

import jax
import jax.numpy as jnp
from jax import lax
from jax.experimental import pallas as pl
from jax.experimental.pallas import tpu as pltpu
from jax.sharding import PartitionSpec as P

HEAD_SIZE = 64
LANES = 128
MESH = pl.DeviceIdType.MESH

masked_score = -1e30
exp2_scale = math.log2(math.e) / math.sqrt(HEAD_SIZE)


def kernel(
    n_ctx, n_head, members, reach_start,
    bounds_ref, q_hbm, k_hbm, v_hbm, out_ref,
    q_in, k_in, v_in, kv_own, q_buf, kv_buf, key_even, key_odd, value_even, value_odd,
    doc_start, bias, top, acc, o_buf,
    in_sem, kv_send, q_send, slab_send, o_send, kv_recv, q_recv, o_recv,
):
    rows = q_in.shape[0]
    group_cols = q_in.shape[1] // members
    tiles = group_cols // LANES
    slab = rows * members
    half = slab // 2
    span = members // n_head
    planes = n_ctx // span
    my_ctx, my_head = lax.axis_index("ctx"), lax.axis_index("head")
    plane = my_ctx // span
    member = lax.rem(my_ctx, span) * n_head + my_head
    reach_slab, reach_row = reach_start // slab, reach_start % slab

    def at(plane_index, member_index):
        return (plane_index * span + member_index // n_head, lax.rem(member_index, n_head))

    def partner(turn):
        return lax.rem(member + turn, members)

    loads = [
        pltpu.make_async_copy(k_hbm, k_in, in_sem.at[0]),
        pltpu.make_async_copy(v_hbm, v_in, in_sem.at[1]),
        pltpu.make_async_copy(q_hbm, q_in, in_sem.at[2]),
    ]
    for load in loads:
        load.start()

    barrier = pltpu.get_barrier_semaphore()
    for turn in range(1, members):
        pl.semaphore_signal(barrier, inc=1, device_id=at(plane, partner(turn)), device_id_type=MESH)
    for step in range(1, planes):
        other = lax.rem(plane + step, planes)
        pl.semaphore_signal(barrier, inc=1, device_id=at(other, member), device_id_type=MESH)

    def low_lanes(count):
        return lax.broadcasted_iota(jnp.int32, (count, LANES), 1) < HEAD_SIZE

    loads[0].wait()
    loads[1].wait()
    low = low_lanes(rows)
    for pair in range(members // 2):
        columns = slice(pair * LANES, (pair + 1) * LANES)
        keys = k_in[:, columns].astype(jnp.float32)
        values = v_in[:, columns].astype(jnp.float32)
        kv_own[2 * pair] = jnp.where(low, keys, pltpu.roll(values, HEAD_SIZE, 1)).astype(jnp.bfloat16)
        kv_own[2 * pair + 1] = jnp.where(low, pltpu.roll(keys, HEAD_SIZE, 1), values).astype(jnp.bfloat16)
    loads[2].wait()

    pl.semaphore_wait(barrier, members - 1 + planes - 1)

    my_rows = pl.ds(pl.multiple_of(member * rows, rows), rows)
    kv_copies, q_copies = [], []
    for turn in range(1, members):
        to = partner(turn)
        copy = pltpu.make_async_remote_copy(
            src_ref=kv_own.at[to],
            dst_ref=kv_buf.at[plane, my_rows],
            send_sem=kv_send.at[turn - 1],
            recv_sem=kv_recv.at[plane],
            device_id=at(plane, to),
            device_id_type=MESH,
        )
        copy.start()
        kv_copies.append(copy)
    pltpu.make_async_copy(kv_own.at[member], kv_buf.at[plane, my_rows], kv_recv.at[plane]).start()
    for turn in range(1, members):
        to = partner(turn)
        copy = pltpu.make_async_remote_copy(
            src_ref=q_in.at[:, pl.ds(pl.multiple_of(to * group_cols, LANES), group_cols)],
            dst_ref=q_buf.at[my_rows],
            send_sem=q_send.at[turn - 1],
            recv_sem=q_recv,
            device_id=at(plane, to),
            device_id_type=MESH,
        )
        copy.start()
        q_copies.append(copy)
    pltpu.make_async_copy(
        q_in.at[:, pl.ds(pl.multiple_of(member * group_cols, LANES), group_cols)],
        q_buf.at[my_rows],
        q_recv,
    ).start()

    position = plane * slab + lax.broadcasted_iota(jnp.int32, (slab, LANES), 0)
    start = jnp.zeros((slab, LANES), jnp.int32)
    for doc in range(1, bounds_ref.shape[0] - 1):
        bound = bounds_ref[doc]
        start = jnp.where(position >= bound, bound, start)
    doc_start[...] = start

    def fill_bias(first_key, count, causal):
        for block in range(2):
            here = slice(block * half, (block + 1) * half)
            key = first_key + lax.broadcasted_iota(jnp.int32, (half, count), 1)
            allowed = key >= jnp.tile(doc_start[here], (1, count // LANES))
            if causal:
                query = plane * slab + block * half + lax.broadcasted_iota(jnp.int32, (half, count), 0)
                allowed = allowed & (key <= query)
            bias[here, :count] = jnp.where(allowed, 0.0, masked_score)

    fill_bias(plane * slab, slab, True)

    pltpu.make_async_copy(kv_buf.at[plane], kv_buf.at[plane], kv_recv.at[plane]).wait()

    def slab_copy(step, first_row):
        piece = kv_buf.at[plane] if first_row == 0 else kv_buf.at[plane, pl.ds(first_row, slab - first_row)]
        return pltpu.make_async_remote_copy(
            src_ref=piece,
            dst_ref=piece,
            send_sem=slab_send.at[step - 1],
            recv_sem=kv_recv.at[plane],
            device_id=at(plane + step, member),
            device_id_type=MESH,
        )

    def each_slab_copy(act):
        for step in range(1, planes):
            to = plane + step
            if reach_start == 0:
                pl.when(to < planes)(lambda: act(slab_copy(step, 0)))
            else:
                early = to < planes // 2
                later = plane > reach_slab if reach_row else plane >= reach_slab
                pl.when((to < planes) & (early | later))(lambda: act(slab_copy(step, 0)))
                if reach_row:
                    part = (to < planes) & (to >= planes // 2) & (plane == reach_slab)
                    pl.when(part)(lambda: act(slab_copy(step, reach_row)))

    each_slab_copy(lambda copy: copy.start())

    def spread(source, first_row):
        count = slab - first_row
        low = low_lanes(count)
        kv = kv_buf[source, first_row:].astype(jnp.float32)
        swapped = pltpu.roll(kv, HEAD_SIZE, 1)
        key_even[:count] = jnp.where(low, kv, 0.0).astype(jnp.bfloat16)
        key_odd[:count] = jnp.where(low, 0.0, swapped).astype(jnp.bfloat16)
        value_even[:count] = jnp.where(low, swapped, 1.0).astype(jnp.bfloat16)
        value_odd[:count] = jnp.where(low, 1.0, kv).astype(jnp.bfloat16)

    def attend(tile, block, count, opening):
        here = slice(block * half, (block + 1) * half)
        queries = q_buf[here, pl.ds(pl.multiple_of(tile * LANES, LANES), LANES)]
        for parity, (key, value) in enumerate(((key_even, value_even), (key_odd, value_odd))):
            scores = lax.dot_general(
                queries, key[:count], (((1,), (1,)), ((), ())), preferred_element_type=jnp.float32
            ) + bias[here, :count]
            peak = jnp.max(scores, axis=1, keepdims=True)
            if opening:
                new_top = jnp.broadcast_to(peak, (half, LANES))
            else:
                old_top = top[tile, parity, here]
                new_top = jnp.maximum(old_top, peak)
            weights = jnp.exp2((scores - jnp.tile(new_top, (1, count // LANES))) * exp2_scale)
            mixed = jnp.dot(
                weights.astype(jnp.bfloat16), value[:count], preferred_element_type=jnp.float32
            )
            if not opening:
                mixed = mixed + acc[tile, parity, here] * jnp.exp2((old_top - new_top) * exp2_scale)
            top[tile, parity, here] = new_top
            acc[tile, parity, here] = mixed

    spread(plane, 0)
    pltpu.make_async_copy(q_buf, q_buf, q_recv).wait()

    @pl.loop(0, tiles)
    def _(tile):
        attend(tile, 0, half, True)
        attend(tile, 1, slab, True)

    def fold(source, first_row):
        piece = kv_buf.at[source] if first_row == 0 else kv_buf.at[source, pl.ds(first_row, slab - first_row)]
        fill_bias(source * slab + first_row, slab - first_row, False)
        pltpu.make_async_copy(piece, piece, kv_recv.at[source]).wait()
        spread(source, first_row)

        @pl.loop(0, tiles)
        def _(tile):
            for block in range(2):
                attend(tile, block, slab - first_row, False)

    if reach_start == 0:
        whole_slabs = plane
    else:
        kept = plane - reach_slab - (1 if reach_row else 0)
        whole_slabs = jnp.where(plane < planes // 2, plane, kept)

    @pl.loop(0, whole_slabs)
    def _(back):
        fold(plane - 1 - back, 0)

    if reach_row:
        pl.when(plane >= planes // 2)(lambda: fold(reach_slab, reach_row))

    low = low_lanes(slab)
    for tile in range(tiles):
        even, odd = acc[tile, 0], acc[tile, 1]
        total = pltpu.roll(jnp.where(low, odd, even), HEAD_SIZE, 1)
        o_buf[:, tile * LANES:(tile + 1) * LANES] = (jnp.where(low, even, odd) / total).astype(jnp.bfloat16)

    my_columns = pl.ds(pl.multiple_of(member * group_cols, LANES), group_cols)
    o_copies = []
    for turn in range(1, members):
        to = partner(turn)
        copy = pltpu.make_async_remote_copy(
            src_ref=o_buf.at[pl.ds(pl.multiple_of(to * rows, rows), rows)],
            dst_ref=out_ref.at[:, my_columns],
            send_sem=o_send.at[turn - 1],
            recv_sem=o_recv,
            device_id=at(plane, to),
            device_id_type=MESH,
        )
        copy.start()
        o_copies.append(copy)
    pltpu.make_async_copy(o_buf.at[my_rows], out_ref.at[:, my_columns], o_recv).start()

    for copy in kv_copies + q_copies:
        copy.wait_send()
    each_slab_copy(lambda copy: copy.wait_send())
    for copy in o_copies:
        copy.wait_send()
    pltpu.make_async_copy(out_ref, out_ref, o_recv).wait()


def exchange(n_ctx, n_head, reach_start, collective_id, queries, keys, values, doc_bounds):
    rows, query_cols = queries.shape
    members = keys.shape[1] // HEAD_SIZE
    group_cols = query_cols // members
    slab = rows * members
    planes = n_ctx * n_head // members
    tiles = group_cols // LANES
    bf16, f32 = jnp.bfloat16, jnp.float32
    dma = pltpu.SemaphoreType.DMA
    return pl.pallas_call(
        functools.partial(kernel, n_ctx, n_head, members, reach_start),
        out_shape=jax.ShapeDtypeStruct((rows, query_cols), bf16),
        in_specs=[pl.BlockSpec(memory_space=pltpu.SMEM)] + [pl.BlockSpec(memory_space=pl.ANY)] * 3,
        out_specs=pl.BlockSpec(memory_space=pl.ANY),
        scratch_shapes=[
            pltpu.VMEM((rows, query_cols), bf16),
            pltpu.VMEM(keys.shape, bf16),
            pltpu.VMEM(values.shape, bf16),
            pltpu.VMEM((members, rows, LANES), bf16),
            pltpu.VMEM((slab, group_cols), bf16),
            pltpu.VMEM((planes, slab, LANES), bf16),
            pltpu.VMEM((slab, LANES), bf16),
            pltpu.VMEM((slab, LANES), bf16),
            pltpu.VMEM((slab, LANES), bf16),
            pltpu.VMEM((slab, LANES), bf16),
            pltpu.VMEM((slab, LANES), jnp.int32),
            pltpu.VMEM((slab, slab), f32),
            pltpu.VMEM((tiles, 2, slab, LANES), f32),
            pltpu.VMEM((tiles, 2, slab, LANES), f32),
            pltpu.VMEM((slab, group_cols), bf16),
            dma((3,)),
            dma((members - 1,)),
            dma((members - 1,)),
            dma((planes - 1,)),
            dma((members - 1,)),
            dma((planes,)),
            dma,
            dma,
        ],
        compiler_params=pltpu.CompilerParams(collective_id=collective_id, has_side_effects=True),
    )(doc_bounds, queries, keys, values)


def solution(mesh):
    n_ctx, n_head = mesh.shape["ctx"], mesh.shape["head"]

    def on_device(queries, keys, values, doc_bounds):
        return exchange(n_ctx, n_head, 0, 0, queries, keys, values, doc_bounds)

    return jax.shard_map(
        on_device,
        mesh=mesh,
        in_specs=(P(("ctx", "head"), None),) * 3 + (P(),),
        out_specs=P(("ctx", "head"), None),
        check_vma=False,
    )
```

time: 88.2 us -> 33.7 us (0.38)
  the two profiles are of different devices: /device:TPU:0 before, /device:TPU:25 now
where the time goes in v1:
time: 33.7 us; the launch traced here: 33.3 us
  Pallas kernels  31.7 us (94%)
  local copies, waits for them, and re-layouts  1.67 us (5%)
    pallas_call x1, Pallas kernels, exchange(): pl.pallas_call(functools.partial(kernel, n_ctx, n_head, members, reach_st...  31.7 us
    unnamed x1, local copies, waits for them, and re-layouts  1.67 us

profile of v1, /device:TPU:25, one launch (start us, length us, event | category | flops | bytes accessed | tf_op | source)
XLA Modules:
  0.0 33.3 jit_solution(14390280210923129469)
XLA Ops:
  0.0 31.7 %shard_map.46 = bf16[64,2048]{1,0:T(8,128)(2,1)} custom-call(s32[17]{0:T(128)} %bounds_ref.1, bf16[64,2048]{1,0:T(8,128)(2,1)} %q_hbm.1, bf16[64,512]{1,0:T(8,128)(2,1)} %k_hbm.1, bf16[64,512]{1,0:T(8,128)(2,1)} %v_hbm.1), custom_call_target="tpu_custom_call" | custom-call | tf_op jit(solution)/shard_map/pallas_call | solution.py:258
  31.7 1.7 %copy.6 = bf16[64,2048]{1,0:T(8,128)(2,1)} copy(bf16[64,2048]{1,0:T(8,128)(2,1)} %shard_map.46) | data formatting | bytes 524288

commit v2 on v1

--- a/solution.py
+++ b/solution.py
@@ -293,7 +293,16 @@
     n_ctx, n_head = mesh.shape["ctx"], mesh.shape["head"]
 
     def on_device(queries, keys, values, doc_bounds):
-        return exchange(n_ctx, n_head, 0, 0, queries, keys, values, doc_bounds)
+        tokens = n_ctx * n_head * queries.shape[0]
+        reach_start = 3 * tokens // 8
+
+        def near(*arrays):
+            return exchange(n_ctx, n_head, reach_start, 0, *arrays)
+
+        def far(*arrays):
+            return exchange(n_ctx, n_head, 0, 1, *arrays)
+
+        return lax.cond(doc_bounds[-2] >= reach_start, near, far, queries, keys, values, doc_bounds)
 
     return jax.shard_map(
         on_device,

time: 33.7 us -> 26.7 us (0.79)
  the two profiles are of different devices: /device:TPU:25 before, /device:TPU:29 now
where the time goes in v2:
time: 26.7 us; the launch traced here: 26.6 us
  Pallas kernels  23.3 us (87%)
  local copies, waits for them, and re-layouts  2.59 us (10%)
  between operations  0.67 us (3%)
    pallas_call x1, Pallas kernels, exchange(): pl.pallas_call(functools.partial(kernel, n_ctx, n_head, members, reach_st...  23.3 us
    unnamed x3, local copies, waits for them, and re-layouts  1.36 us
    slice x1, local copies, waits for them, and re-layouts, on_device(): doc_bounds[-2] >= reach_start  1.24 us

profile of v2, /device:TPU:29, one launch (start us, length us, event | category | flops | bytes accessed | tf_op | source)
XLA Modules:
  0.0 26.6 jit_solution(15099597061476165484)
XLA Ops:
  0.0 1.2 %slice.3 = s32[1]{0:T(128)} slice(s32[17]{0:T(128)} %param.9), slice={[15:16]} | slice | bytes 8 | tf_op jit(solution)/shard_map/slice | solution.py:305
  1.9 0.0 copy-start
  1.9 0.6 %copy-done = s32[17]{0:T(128)S(1)} copy-done((s32[17]{0:T(128)S(1)}, s32[17]{0:T(128)}, u32[]{:S(2)}) %copy-start) | copy-done | bytes 92
  2.5 23.3 %conditional.1 = (bf16[64,2048]{1,0:T(8,128)(2,1)S(1)}) conditional(s32[]{:T(128)} %bitcast, (s32[17]{0:T(128)S(1)}, bf16[64,2048]{1,0:T(8,128)(2,1)}, bf16[64,512]{1,0:T(8,128)(2,1)}, bf16[64,512]{1,0:T(8,128)(2,1)}) %tuple.16, (s32[17]{0:T(128)S(1)}, bf16[64,2048]{1,0:T(8,128)(2,1)}, bf16[64,512]{1,0:T(8,128)(2,1)}, bf16[64,512]{1,0:T(8,128)(2,1)}) %tuple.17), branch_computations={%region_0.0_spmd, %region_1.0_spmd} | conditional | bytes 8 | solution.py:305
  2.5 23.3 %branch_1_fun.1 = bf16[64,2048]{1,0:T(8,128)(2,1)S(1)} custom-call(s32[17]{0:T(128)S(1)} %get-tuple-element.28.bounds_ref, bf16[64,2048]{1,0:T(8,128)(2,1)} %get-tuple-element.40.q_hbm, bf16[64,512]{1,0:T(8,128)(2,1)} %get-tuple-element.42.k_hbm, bf16[64,512]{1,0:T(8,128)(2,1)} %get-tuple-element.44.v_hbm), custom_call_target="tpu_custom_call" | custom-call | tf_op jit(solution)/shard_map/cond/branch_1_fun/pallas_call | solution.py:258
  25.8 0.7 %copy.16 = bf16[64,2048]{1,0:T(8,128)(2,1)} copy(bf16[64,2048]{1,0:T(8,128)(2,1)S(1)} %get-tuple-element.32) | data formatting | bytes 524288
Async XLA Ops:
  1.9 0.7 %copy-start = (s32[17]{0:T(128)S(1)}, s32[17]{0:T(128)}, u32[]{:S(2)}) copy-start(s32[17]{0:T(128)} %param.9) | copy-start | bytes 208

commit v3 on v2

--- a/solution.py
+++ b/solution.py
@@ -21,7 +21,7 @@
     bounds_ref, q_hbm, k_hbm, v_hbm, out_ref,
     q_in, k_in, v_in, kv_own, q_buf, kv_buf, key_even, key_odd, value_even, value_odd,
     doc_start, bias, top, acc, o_buf,
-    in_sem, kv_send, q_send, slab_send, o_send, kv_recv, q_recv, o_recv,
+    in_sem, kv_send, q_send, slab_send, o_send, kv_recv, q_recv, o_recv, ready,
 ):
     rows = q_in.shape[0]
     group_cols = q_in.shape[1] // members
@@ -53,8 +53,11 @@
     for turn in range(1, members):
         pl.semaphore_signal(barrier, inc=1, device_id=at(plane, partner(turn)), device_id_type=MESH)
     for step in range(1, planes):
-        other = lax.rem(plane + step, planes)
-        pl.semaphore_signal(barrier, inc=1, device_id=at(other, member), device_id_type=MESH)
+        @pl.when(plane + step < planes)
+        def _():
+            pl.semaphore_signal(
+                barrier, inc=1, device_id=at(plane + step, member), device_id_type=MESH
+            )
 
     def low_lanes(count):
         return lax.broadcasted_iota(jnp.int32, (count, LANES), 1) < HEAD_SIZE
@@ -70,7 +73,13 @@
         kv_own[2 * pair + 1] = jnp.where(low, pltpu.roll(keys, HEAD_SIZE, 1), values).astype(jnp.bfloat16)
     loads[2].wait()
 
-    pl.semaphore_wait(barrier, members - 1 + planes - 1)
+    pl.semaphore_wait(barrier, members - 1 + plane)
+    for step in range(1, planes):
+        @pl.when(plane >= step)
+        def _():
+            pl.semaphore_signal(
+                ready, inc=1, device_id=at(plane - step, member), device_id_type=MESH
+            )
 
     my_rows = pl.ds(pl.multiple_of(member * rows, rows), rows)
     kv_copies, q_copies = [], []
@@ -87,23 +96,25 @@
         copy.start()
         kv_copies.append(copy)
     pltpu.make_async_copy(kv_own.at[member], kv_buf.at[plane, my_rows], kv_recv.at[plane]).start()
-    for turn in range(1, members):
-        to = partner(turn)
-        copy = pltpu.make_async_remote_copy(
-            src_ref=q_in.at[:, pl.ds(pl.multiple_of(to * group_cols, LANES), group_cols)],
-            dst_ref=q_buf.at[my_rows],
-            send_sem=q_send.at[turn - 1],
-            recv_sem=q_recv,
-            device_id=at(plane, to),
-            device_id_type=MESH,
-        )
-        copy.start()
-        q_copies.append(copy)
-    pltpu.make_async_copy(
-        q_in.at[:, pl.ds(pl.multiple_of(member * group_cols, LANES), group_cols)],
-        q_buf.at[my_rows],
-        q_recv,
-    ).start()
+    for tile in range(tiles):
+        def query_columns(owner):
+            return pl.ds(pl.multiple_of(owner * group_cols + tile * LANES, LANES), LANES)
+
+        for turn in range(1, members):
+            to = partner(turn)
+            copy = pltpu.make_async_remote_copy(
+                src_ref=q_in.at[:, query_columns(to)],
+                dst_ref=q_buf.at[tile, my_rows],
+                send_sem=q_send.at[tile, turn - 1],
+                recv_sem=q_recv.at[tile],
+                device_id=at(plane, to),
+                device_id_type=MESH,
+            )
+            copy.start()
+            q_copies.append(copy)
+        pltpu.make_async_copy(
+            q_in.at[:, query_columns(member)], q_buf.at[tile, my_rows], q_recv.at[tile]
+        ).start()
 
     position = plane * slab + lax.broadcasted_iota(jnp.int32, (slab, LANES), 0)
     start = jnp.zeros((slab, LANES), jnp.int32)
@@ -112,17 +123,18 @@
         start = jnp.where(position >= bound, bound, start)
     doc_start[...] = start
 
-    def fill_bias(first_key, count, causal):
+    def fill_bias(slab_start, first, last, causal):
+        count = last - first
         for block in range(2):
             here = slice(block * half, (block + 1) * half)
-            key = first_key + lax.broadcasted_iota(jnp.int32, (half, count), 1)
+            key = slab_start + first + lax.broadcasted_iota(jnp.int32, (half, count), 1)
             allowed = key >= jnp.tile(doc_start[here], (1, count // LANES))
             if causal:
                 query = plane * slab + block * half + lax.broadcasted_iota(jnp.int32, (half, count), 0)
                 allowed = allowed & (key <= query)
-            bias[here, :count] = jnp.where(allowed, 0.0, masked_score)
-
-    fill_bias(plane * slab, slab, True)
+            bias[here, first:last] = jnp.where(allowed, 0.0, masked_score)
+
+    fill_bias(plane * slab, 0, slab, True)
 
     pltpu.make_async_copy(kv_buf.at[plane], kv_buf.at[plane], kv_recv.at[plane]).wait()
 
@@ -150,25 +162,29 @@
                     part = (to < planes) & (to >= planes // 2) & (plane == reach_slab)
                     pl.when(part)(lambda: act(slab_copy(step, reach_row)))
 
+    pl.when(plane < planes - 1)(lambda: pl.semaphore_wait(ready, planes - 1 - plane))
     each_slab_copy(lambda copy: copy.start())
 
     def spread(source, first_row):
-        count = slab - first_row
-        low = low_lanes(count)
+        low = low_lanes(slab - first_row)
         kv = kv_buf[source, first_row:].astype(jnp.float32)
         swapped = pltpu.roll(kv, HEAD_SIZE, 1)
-        key_even[:count] = jnp.where(low, kv, 0.0).astype(jnp.bfloat16)
-        key_odd[:count] = jnp.where(low, 0.0, swapped).astype(jnp.bfloat16)
-        value_even[:count] = jnp.where(low, swapped, 1.0).astype(jnp.bfloat16)
-        value_odd[:count] = jnp.where(low, 1.0, kv).astype(jnp.bfloat16)
-
-    def attend(tile, block, count, opening):
+        key_even[source, first_row:] = jnp.where(low, kv, 0.0).astype(jnp.bfloat16)
+        key_odd[source, first_row:] = jnp.where(low, 0.0, swapped).astype(jnp.bfloat16)
+        value_even[source, first_row:] = jnp.where(low, swapped, 1.0).astype(jnp.bfloat16)
+        value_odd[source, first_row:] = jnp.where(low, 1.0, kv).astype(jnp.bfloat16)
+
+    def attend(tile, block, source, keys, opening, masked):
         here = slice(block * half, (block + 1) * half)
-        queries = q_buf[here, pl.ds(pl.multiple_of(tile * LANES, LANES), LANES)]
+        count = keys.stop - keys.start
+        queries = q_buf[tile, here]
         for parity, (key, value) in enumerate(((key_even, value_even), (key_odd, value_odd))):
             scores = lax.dot_general(
-                queries, key[:count], (((1,), (1,)), ((), ())), preferred_element_type=jnp.float32
-            ) + bias[here, :count]
+                queries, key[source, keys], (((1,), (1,)), ((), ())),
+                preferred_element_type=jnp.float32,
+            )
+            if masked:
+                scores = scores + bias[here, keys]
             peak = jnp.max(scores, axis=1, keepdims=True)
             if opening:
                 new_top = jnp.broadcast_to(peak, (half, LANES))
@@ -177,7 +193,8 @@
                 new_top = jnp.maximum(old_top, peak)
             weights = jnp.exp2((scores - jnp.tile(new_top, (1, count // LANES))) * exp2_scale)
             mixed = jnp.dot(
-                weights.astype(jnp.bfloat16), value[:count], preferred_element_type=jnp.float32
+                weights.astype(jnp.bfloat16), value[source, keys],
+                preferred_element_type=jnp.float32,
             )
             if not opening:
                 mixed = mixed + acc[tile, parity, here] * jnp.exp2((old_top - new_top) * exp2_scale)
@@ -185,64 +202,73 @@
             acc[tile, parity, here] = mixed
 
     spread(plane, 0)
-    pltpu.make_async_copy(q_buf, q_buf, q_recv).wait()
-
-    @pl.loop(0, tiles)
-    def _(tile):
-        attend(tile, 0, half, True)
-        attend(tile, 1, slab, True)
-
-    def fold(source, first_row):
-        piece = kv_buf.at[source] if first_row == 0 else kv_buf.at[source, pl.ds(first_row, slab - first_row)]
-        fill_bias(source * slab + first_row, slab - first_row, False)
-        pltpu.make_async_copy(piece, piece, kv_recv.at[source]).wait()
-        spread(source, first_row)
-
-        @pl.loop(0, tiles)
-        def _(tile):
-            for block in range(2):
-                attend(tile, block, slab - first_row, False)
-
+    for tile in range(tiles):
+        pltpu.make_async_copy(q_buf.at[tile], q_buf.at[tile], q_recv.at[tile]).wait()
+        attend(tile, 0, plane, slice(0, half), True, True)
+        attend(tile, 1, plane, slice(0, slab), True, True)
+
+    def fold(tile, source, first_row, masked):
+        if masked:
+            fill_bias(source * slab, first_row, slab, False)
+
+        @pl.when(tile == 0)
+        def _():
+            piece = kv_buf.at[source] if first_row == 0 else kv_buf.at[source, pl.ds(first_row, slab - first_row)]
+            pltpu.make_async_copy(piece, piece, kv_recv.at[source]).wait()
+            spread(source, first_row)
+
+        for block in range(2):
+            attend(tile, block, source, slice(first_row, slab), False, masked)
+
+    middle = planes // 2
+    clear_slabs = jnp.maximum(plane - middle, 0)
     if reach_start == 0:
         whole_slabs = plane
     else:
         kept = plane - reach_slab - (1 if reach_row else 0)
-        whole_slabs = jnp.where(plane < planes // 2, plane, kept)
-
-    @pl.loop(0, whole_slabs)
-    def _(back):
-        fold(plane - 1 - back, 0)
-
-    if reach_row:
-        pl.when(plane >= planes // 2)(lambda: fold(reach_slab, reach_row))
-
-    low = low_lanes(slab)
-    for tile in range(tiles):
+        whole_slabs = jnp.where(plane < middle, plane, kept)
+
+    def out_copies(tile):
+        columns = pl.ds(pl.multiple_of(member * group_cols + tile * LANES, LANES), LANES)
+        for turn in range(1, members):
+            to = partner(turn)
+            yield pltpu.make_async_remote_copy(
+                src_ref=o_buf.at[tile, pl.ds(pl.multiple_of(to * rows, rows), rows)],
+                dst_ref=out_ref.at[:, columns],
+                send_sem=o_send.at[tile, turn - 1],
+                recv_sem=o_recv,
+                device_id=at(plane, to),
+                device_id_type=MESH,
+            )
+
+    @pl.loop(0, tiles)
+    def _(tile):
+        @pl.loop(0, clear_slabs)
+        def _(back):
+            fold(tile, plane - 1 - back, 0, False)
+
+        @pl.loop(clear_slabs, whole_slabs)
+        def _(back):
+            fold(tile, plane - 1 - back, 0, True)
+
+        if reach_row:
+            pl.when(plane >= middle)(lambda: fold(tile, reach_slab, reach_row, True))
+
+        low = low_lanes(slab)
         even, odd = acc[tile, 0], acc[tile, 1]
         total = pltpu.roll(jnp.where(low, odd, even), HEAD_SIZE, 1)
-        o_buf[:, tile * LANES:(tile + 1) * LANES] = (jnp.where(low, even, odd) / total).astype(jnp.bfloat16)
-
-    my_columns = pl.ds(pl.multiple_of(member * group_cols, LANES), group_cols)
-    o_copies = []
-    for turn in range(1, members):
-        to = partner(turn)
-        copy = pltpu.make_async_remote_copy(
-            src_ref=o_buf.at[pl.ds(pl.multiple_of(to * rows, rows), rows)],
-            dst_ref=out_ref.at[:, my_columns],
-            send_sem=o_send.at[turn - 1],
-            recv_sem=o_recv,
-            device_id=at(plane, to),
-            device_id_type=MESH,
-        )
-        copy.start()
-        o_copies.append(copy)
-    pltpu.make_async_copy(o_buf.at[my_rows], out_ref.at[:, my_columns], o_recv).start()
+        o_buf[tile] = (jnp.where(low, even, odd) / total).astype(jnp.bfloat16)
+        for copy in out_copies(tile):
+            copy.start()
+        columns = pl.ds(pl.multiple_of(member * group_cols + tile * LANES, LANES), LANES)
+        pltpu.make_async_copy(o_buf.at[tile, my_rows], out_ref.at[:, columns], o_recv).start()
 
     for copy in kv_copies + q_copies:
         copy.wait_send()
     each_slab_copy(lambda copy: copy.wait_send())
-    for copy in o_copies:
-        copy.wait_send()
+    for tile in range(tiles):
+        for copy in out_copies(tile):
+            copy.wait_send()
     pltpu.make_async_copy(out_ref, out_ref, o_recv).wait()
 
 
@@ -265,25 +291,26 @@
             pltpu.VMEM(keys.shape, bf16),
             pltpu.VMEM(values.shape, bf16),
             pltpu.VMEM((members, rows, LANES), bf16),
-            pltpu.VMEM((slab, group_cols), bf16),
-            pltpu.VMEM((planes, slab, LANES), bf16),
-            pltpu.VMEM((slab, LANES), bf16),
-            pltpu.VMEM((slab, LANES), bf16),
-            pltpu.VMEM((slab, LANES), bf16),
-            pltpu.VMEM((slab, LANES), bf16),
+            pltpu.VMEM((tiles, slab, LANES), bf16),
+            pltpu.VMEM((planes, slab, LANES), bf16),
+            pltpu.VMEM((planes, slab, LANES), bf16),
+            pltpu.VMEM((planes, slab, LANES), bf16),
+            pltpu.VMEM((planes, slab, LANES), bf16),
+            pltpu.VMEM((planes, slab, LANES), bf16),
             pltpu.VMEM((slab, LANES), jnp.int32),
             pltpu.VMEM((slab, slab), f32),
             pltpu.VMEM((tiles, 2, slab, LANES), f32),
             pltpu.VMEM((tiles, 2, slab, LANES), f32),
-            pltpu.VMEM((slab, group_cols), bf16),
+            pltpu.VMEM((tiles, slab, LANES), bf16),
             dma((3,)),
             dma((members - 1,)),
-            dma((members - 1,)),
+            dma((tiles, members - 1)),
             dma((planes - 1,)),
-            dma((members - 1,)),
+            dma((tiles, members - 1)),
             dma((planes,)),
+            dma((tiles,)),
             dma,
-            dma,
+            pltpu.SemaphoreType.REGULAR,
         ],
         compiler_params=pltpu.CompilerParams(collective_id=collective_id, has_side_effects=True),
     )(doc_bounds, queries, keys, values)

time: 26.7 us -> 25.6 us (0.959)
  the two profiles are of different devices: /device:TPU:29 before, /device:TPU:25 now
where the time goes in v3:
time: 25.6 us; the launch traced here: 25.5 us
  Pallas kernels  22 us (86%)
  local copies, waits for them, and re-layouts  2.59 us (10%)
  between operations  0.67 us (3%)
    pallas_call x1, Pallas kernels, exchange(): pl.pallas_call(functools.partial(kernel, n_ctx, n_head, members, reach_st...  22 us
    unnamed x3, local copies, waits for them, and re-layouts  1.36 us
    slice x1, local copies, waits for them, and re-layouts, on_device(): doc_bounds[-2] >= reach_start  1.24 us

profile of v3, /device:TPU:25, one launch (start us, length us, event | category | flops | bytes accessed | tf_op | source)
XLA Modules:
  0.0 25.5 jit_solution(16057854020854233373)
XLA Ops:
  0.0 1.2 %slice.3 = s32[1]{0:T(128)} slice(s32[17]{0:T(128)} %param.9), slice={[15:16]} | slice | bytes 8 | tf_op jit(solution)/shard_map/slice | solution.py:332
  1.9 0.0 copy-start
  1.9 0.6 %copy-done = s32[17]{0:T(128)S(1)} copy-done((s32[17]{0:T(128)S(1)}, s32[17]{0:T(128)}, u32[]{:S(2)}) %copy-start) | copy-done | bytes 92
  2.5 22.2 %conditional.1 = (bf16[64,2048]{1,0:T(8,128)(2,1)S(1)}) conditional(s32[]{:T(128)} %bitcast, (s32[17]{0:T(128)S(1)}, bf16[64,2048]{1,0:T(8,128)(2,1)}, bf16[64,512]{1,0:T(8,128)(2,1)}, bf16[64,512]{1,0:T(8,128)(2,1)}) %tuple.16, (s32[17]{0:T(128)S(1)}, bf16[64,2048]{1,0:T(8,128)(2,1)}, bf16[64,512]{1,0:T(8,128)(2,1)}, bf16[64,512]{1,0:T(8,128)(2,1)}) %tuple.17), branch_computations={%region_0.0_spmd, %region_1.0_spmd} | conditional | bytes 8 | solution.py:332
  2.5 22.0 %branch_1_fun.1 = bf16[64,2048]{1,0:T(8,128)(2,1)S(1)} custom-call(s32[17]{0:T(128)S(1)} %get-tuple-element.28.bounds_ref, bf16[64,2048]{1,0:T(8,128)(2,1)} %get-tuple-element.40.q_hbm, bf16[64,512]{1,0:T(8,128)(2,1)} %get-tuple-element.42.k_hbm, bf16[64,512]{1,0:T(8,128)(2,1)} %get-tuple-element.44.v_hbm), custom_call_target="tpu_custom_call" | custom-call | tf_op jit(solution)/shard_map/cond/branch_1_fun/pallas_call | solution.py:284
  24.8 0.7 %copy.16 = bf16[64,2048]{1,0:T(8,128)(2,1)} copy(bf16[64,2048]{1,0:T(8,128)(2,1)S(1)} %get-tuple-element.32) | data formatting | bytes 524288
Async XLA Ops:
  1.9 0.7 %copy-start = (s32[17]{0:T(128)S(1)}, s32[17]{0:T(128)}, u32[]{:S(2)}) copy-start(s32[17]{0:T(128)} %param.9) | copy-start | bytes 208
